TPU v7x, 32 devices: a whole 2x2x4 slice. The times are simulated.
32 devices in a mesh: dp: 8 (over z, y), tensor: 4 (over x, core).
Axes of the slice: x: 2, y: 2, z: 4, core: 2. Of those that a mesh axis runs over, the one named last changes fastest.
Arguments:
- acts: bfloat16 [8192, 5120], P('dp', 'tensor'), may hold values from -6 to 6
- out_grad: bfloat16 [8192, 2048], P(('dp', 'tensor')), may hold values from -0.1875 to 0.1875
- momentum: float32 [40960, 2048], P(('dp', 'tensor')), may hold values from -100 to 100
- q_basis: float32 [2048, 256], P('tensor'), may hold values from -0.125 to 0.125
Outputs:
- new_momentum: float32 [40960, 2048], P(('dp', 'tensor'))
- ortho: float32 [5120, 256], P('tensor')
- new_q: float32 [2048, 256], P('tensor')
All inputs are finite; a program needn't handle non-finite values.
Results may differ from a plain program's by a relative error of at most 0.0003.
Values may be sent and summed in bfloat16 or wider, within the bound.
No kernel may reach another device: no remote copies, remote signals or barrier semaphores. Data moves between devices by JAX's collectives and lax.ppermute only.
A program may use at most 64 MiB of HBM per device.

v0:
```python
import jax
import jax.numpy as jnp
from jax import lax
from jax.sharding import PartitionSpec as P

HIGH = lax.Precision.HIGHEST


def contract_rows(first, second):
    return lax.dot_general(
        first, second, (((0,), (0,)), ((), ())), precision=HIGH, preferred_element_type=jnp.float32
    )


def orthonormal(left, gram):
    chol = jnp.linalg.cholesky(gram)
    return lax.linalg.triangular_solve(chol, left, left_side=False, lower=True, transpose_a=True)


def body(acts, out_grad, momentum, q_basis):
    replicas = lax.axis_size("dp")
    grad = lax.dot_general(
        acts,
        lax.all_gather(out_grad, "tensor", axis=0, tiled=True),
        (((0,), (0,)), ((), ())),
        preferred_element_type=jnp.float32,
    )
    buffer = 0.95 * momentum + grad
    columns = buffer
    left_local = jnp.dot(
        columns,
        lax.all_gather(q_basis, "tensor", axis=0, tiled=True),
        precision=HIGH,
        preferred_element_type=jnp.float32,
    )
    left = lax.psum(left_local, "dp") / replicas
    gram = lax.psum(contract_rows(left, left), "tensor")
    ortho = orthonormal(left, gram)
    columns = buffer
    right_share = lax.psum_scatter(
        contract_rows(columns, ortho), "tensor", scatter_dimension=0, tiled=True
    )
    right_share = lax.psum(right_share, "dp") / replicas
    col_squares = lax.psum(jnp.sum(right_share * right_share, axis=0, keepdims=True), "tensor")
    new_q = right_share * lax.rsqrt(col_squares + 1e-06)
    columns = buffer
    update = lax.dot_general(
        ortho,
        lax.all_gather(right_share.astype(jnp.bfloat16), "tensor", axis=0, tiled=True).astype(
            jnp.float32
        ),
        (((1,), (1,)), ((), ())),
        precision=HIGH,
        preferred_element_type=jnp.float32,
    )
    new_momentum = columns - 0.05 * update
    return (new_momentum, ortho, new_q)


def solution(mesh):
    in_specs = (
        P("dp", "tensor"),
        P(("dp", "tensor"), None),
        P(("dp", "tensor"), None),
        P("tensor", None),
    )
    out_specs = (P(("dp", "tensor"), None), P("tensor", None), P("tensor", None))
    return jax.shard_map(body, mesh=mesh, in_specs=in_specs, out_specs=out_specs, check_vma=False)
```

profile of v0, /device:TPU:0, one launch (start us, length us, event | category | flops | bytes accessed | tf_op | source)
XLA Modules:
  0.0 450.5 jit_solution(18422451597590470659)
XLA Ops:
  7.2 0.0 all-gather.4.cloned.1.call-start
  7.2 0.7 all-gather.4.cloned.1.call-update
  7.9 0.0 all-gather.6.cloned.1.call-start
  8.0 0.7 all-gather.6.cloned.1.call-update
  8.7 0.0 all-reduce.5.cloned.1.call-start
  8.7 38.0 %all-gather.4.cloned.1.call-done = bf16[1024,2048]{1,0:T(8,128)(2,1)} async-done(((bf16[256,2048]{1,0:T(8,128)(2,1)}), bf16[1024,2048]{1,0:T(8,128)(2,1)}) %all-gather.4.cloned.1.call-update) | async-done | bytes 4194320 | tf_op jit(solution)/shard_map/all_gather | solution.py:24
  46.8 12.1 %multiply_add_fusion = f32[1280,2048]{1,0:T(8,128)} fusion(f32[1280,2048]{1,0:T(8,128)} %param.6, bf16[1024,1280]{1,0:T(8,128)(2,1)S(1)} %copy-done, bf16[1024,2048]{1,0:T(8,128)(2,1)} %all-gather.4.cloned.1.call-done), kind=kOutput, calls=%fused_computation.3 | convolution fusion | flops 5373952000 | bytes 27787264 | tf_op jit(solution)/shard_map/dot_general | solution.py:22
  58.9 12.0 %all-gather.6.cloned.1.call-done = f32[2048,256]{1,0:T(8,128)} async-done(((f32[512,256]{1,0:T(8,128)}), f32[2048,256]{1,0:T(8,128)}) %all-gather.6.cloned.1.call-update) | async-done | bytes 2097168 | tf_op jit(solution)/shard_map/all_gather | solution.py:32
  70.9 12.5 %fusion.11 = f32[1280,256]{1,0:T(8,128)} fusion(f32[1280,2048]{1,0:T(8,128)} %multiply_add_fusion, f32[2048,256]{1,0:T(8,128)} %all-gather.6.cloned.1.call-done), kind=kOutput, calls=%fused_computation.38 | convolution fusion | flops 8053063680 | bytes 13893632 | tf_op jit(solution)/shard_map/dot_general | solution.py:30
  83.4 0.0 all-reduce.5.cloned.1.call-update
  83.4 0.0 all-reduce.7.cloned.1.call-start
  83.5 83.7 %all-reduce.5.cloned.1.call-done = f32[1280,256]{1,0:T(8,128)} async-done(((f32[1280,256]{1,0:T(8,128)}), f32[1280,256]{1,0:T(8,128)}) %all-reduce.5.cloned.1.call-update) | async-done | bytes 1310736 | tf_op jit(solution)/shard_map/psum | solution.py:36
  167.2 4.8 %fusion.8 = f32[256,256]{0,1:T(8,128)} fusion(f32[1280,256]{1,0:T(8,128)} %all-reduce.5.cloned.1.call-done), kind=kOutput, calls=%fused_computation.35 | convolution fusion | flops 1006960640 | bytes 1572864 | tf_op jit(solution)/shard_map/dot_general | solution.py:10
  172.0 0.5 reduce-scatter.2.cloned.1.call-start
  172.5 2.5 broadcast_multiply_fusion
  175.0 28.5 %all-reduce.7.cloned.1.call-done = f32[256,256]{0,1:T(8,128)} async-done(((f32[256,256]{0,1:T(8,128)}), f32[256,256]{0,1:T(8,128)}) %all-reduce.7.cloned.1.call-update) | async-done | bytes 262160 | tf_op jit(solution)/shard_map/psum | solution.py:37
  203.5 1.1 copy.8
  204.6 1.0 fusion.2
  205.6 11.7 %cholesky.50 = f32[128,128]{1,0:T(8,128)S(1)} custom-call(f32[128,128]{1,0:T(8,128)S(1)} %cholesky.118), custom_call_target="Cholesky" | custom-call | tf_op jit(solution)/shard_map/jit(cholesky)/cholesky | solution.py:16
  217.4 9.8 %custom-call.14 = f32[1,128,128]{1,2,0:T(8,128)S(1)} custom-call(f32[1,128,128]{2,1,0:T(8,128)S(1)} %get-tuple-element.29), custom_call_target="InvertDiagBlocksLowerTriangular" | custom-call | tf_op jit(solution)/shard_map/jit(cholesky)/cholesky | solution.py:16
  227.2 0.2 constant_dynamic-update-slice_fusion.1
  227.4 0.3 convolution_subtract_fusion.1
  227.7 11.7 %cholesky.105 = f32[128,128]{1,0:T(8,128)S(1)} custom-call(f32[128,128]{1,0:T(8,128)S(1)} %convolution_subtract_fusion.1), custom_call_target="Cholesky" | custom-call | tf_op jit(solution)/shard_map/jit(cholesky)/cholesky | solution.py:16
  239.4 0.7 compare_reduce_fusion
  241.4 0.1 triangular_solve.58
  241.5 5.3 %while.1 = (s32[]{:T(128)}, f32[256,256]{1,0:T(8,128)S(1)}, s32[2,2]{1,0:T(2,128)S(1)}, f32[2,128,128]{2,1,0:T(8,128)}, s32[]{:T(128)}) while((s32[]{:T(128)}, f32[256,256]{1,0:T(8,128)S(1)}, s32[2,2]{1,0:T(2,128)S(1)}, f32[2,128,128]{2,1,0:T(8,128)}, s32[]{:T(128)}) %tuple.29), condition=%wide.while_cond, body=%wide.while_body.sunk | while | flops 2 | bytes 132205 | solution.py:17
  241.6 0.6 fusion.23
  242.2 2.0 bitcast_dynamic-update-slice_fusion.2
  244.2 0.6 fusion.23
  244.8 2.0 bitcast_dynamic-update-slice_fusion.2
  246.8 21.1 %custom-call.15 = f32[2,128,128]{1,2,0:T(8,128)} custom-call(f32[2,128,128]{2,1,0:T(8,128)} %get-tuple-element.10), custom_call_target="InvertDiagBlocksLowerTriangular" | custom-call | tf_op jit(solution)/shard_map/triangular_solve | solution.py:17
  267.9 1.8 fusion
  269.8 2.3 convolution_subtract_fusion
  272.1 0.7 fusion.3
  272.8 0.8 copy-done.1
  273.6 20.1 %fusion.9 = f32[2048,256]{1,0:T(8,128)} fusion(f32[1280,2048]{1,0:T(8,128)} %multiply_add_fusion, f32[1280,128]{0,1:T(8,128)S(1)} %fusion.3, f32[1280,128]{0,1:T(8,128)S(1)} %fusion), kind=kOutput, calls=%fused_computation.36 | convolution fusion | flops 8053391360 | bytes 13893632 | tf_op jit(solution)/shard_map/dot_general | solution.py:10
  293.8 0.0 all-reduce.9.cloned.1.call-start
  293.8 31.3 %reduce-scatter.2.cloned.1.call-done = f32[512,256]{1,0:T(8,128)} async-done(((f32[2048,256]{1,0:T(8,128)}), f32[512,256]{1,0:T(8,128)}) %reduce-scatter.2.cloned.1.call-update) | async-done | bytes 524304 | tf_op jit(solution)/shard_map/reduce_scatter | solution.py:40
  325.1 0.0 all-reduce.9.cloned.1.call-update
  325.1 0.0 all-gather.8.cloned.1.call-start
  325.2 76.0 %all-reduce.9.cloned.1.call-done = f32[512,256]{1,0:T(8,128)} async-done(((f32[512,256]{1,0:T(8,128)}), f32[512,256]{1,0:T(8,128)}) %all-reduce.9.cloned.1.call-update) | async-done | bytes 524304 | tf_op jit(solution)/shard_map/psum | solution.py:43
  401.2 1.1 multiply_reduce_fusion
  402.3 5.9 %psum.31 = f32[1,256]{1,0:T(1,128)S(1)} all-reduce(f32[1,256]{1,0:T(1,128)S(1)} %bitcast.39), channel_id=1, replica_groups=mesh['dp'=8,'tensor'=4] {'tensor'}, use_global_device_ids=true, to_apply=%region_9.10 | all-reduce | flops 256 | bytes 2048 | tf_op jit(solution)/shard_map/psum | solution.py:44
  408.2 2.0 broadcast_multiply_fusion.1
  410.2 2.2 pad_maximum_fusion
  412.5 2.8 copy.9
  415.2 11.3 %all-gather.8.cloned.1.call-done = bf16[2048,256]{1,0:T(8,128)(2,1)} async-done(((bf16[512,256]{1,0:T(8,128)(2,1)}), bf16[2048,256]{1,0:T(8,128)(2,1)}) %all-gather.8.cloned.1.call-update) | async-done | bytes 1048592 | tf_op jit(solution)/shard_map/all_gather | solution.py:49
  426.5 17.0 %multiply_subtract_fusion = f32[1280,2048]{1,0:T(8,128)} fusion(f32[1280,2048]{1,0:T(8,128)} %multiply_add_fusion, bf16[2048,256]{1,0:T(8,128)(2,1)} %all-gather.8.cloned.1.call-done, f32[1280,128]{0,1:T(8,128)} %copy-done.1, f32[1280,128]{0,1:T(8,128)S(1)} %fusion), kind=kOutput, calls=%fused_computation.2 | convolution fusion | flops 8058634240 | bytes 23330816 | tf_op jit(solution)/shard_map/dot_general | solution.py:47
  (18 shorter events, 0.2 us)
Async XLA Ops:
  7.2 39.6 %copy-start = (bf16[1024,1280]{1,0:T(8,128)(2,1)S(1)}, bf16[1024,1280]{1,0:T(8,128)(2,1)}, u32[]{:S(2)}) copy-start(bf16[1024,1280]{1,0:T(8,128)(2,1)} %param.4) | copy-start | bytes 7864324
  7.2 39.6 %all-gather.4.cloned.1.call-start = ((), (), s32[]{:S(2)}) async-start(), calls=%async_computation.1 | async-start | bytes 5242880 | tf_op jit(solution)/shard_map/all_gather | solution.py:24
  7.9 63.0 %all-gather.6.cloned.1.call-start = ((), (), s32[]{:S(2)}) async-start(), calls=%async_computation.2 | async-start | bytes 2621440 | tf_op jit(solution)/shard_map/all_gather | solution.py:32
  8.7 158.6 %all-reduce.5.cloned.1.call-start = ((), (), s32[]{:S(2)}) async-start(), calls=%async_computation.3 | async-start | bytes 2621440 | tf_op jit(solution)/shard_map/psum | solution.py:36
  83.4 120.1 %all-reduce.7.cloned.1.call-start = ((), (), s32[]{:S(2)}) async-start(), calls=%async_computation.4 | async-start | bytes 524288 | tf_op jit(solution)/shard_map/psum | solution.py:37
  172.0 153.1 %reduce-scatter.2.cloned.1.call-start = ((), (), s32[]{:S(2)}) async-start(), calls=%async_computation.5 | async-start | bytes 2621440 | tf_op jit(solution)/shard_map/reduce_scatter | solution.py:40
  267.9 4.2 copy-start.2
  272.8 0.8 copy-start.1
  293.8 107.4 %all-reduce.9.cloned.1.call-start = ((), (), s32[]{:S(2)}) async-start(), calls=%async_computation.6 | async-start | bytes 1048576 | tf_op jit(solution)/shard_map/psum | solution.py:43
  325.1 101.4 %all-gather.8.cloned.1.call-start = ((), (), s32[]{:S(2)}) async-start(), calls=%async_computation.7 | async-start | bytes 1310720 | tf_op jit(solution)/shard_map/all_gather | solution.py:49
Sparse Core Ops, SparseCore 0:
  9.5 37.1 all-gather.3
  48.3 22.5 all-gather.5
  83.5 83.6 all-reduce.4
  172.1 31.3 all-reduce.6
  293.9 31.1 reduce-scatter.1
  328.4 72.7 all-reduce.8
  410.3 16.1 all-gather.7
where the time goes:
time: 458 us; the launch traced here: 451 us
  waiting for transfers between devices  282 us (62%)
  matrix products  71.8 us (16%)
  other arithmetic  63.9 us (14%)
  between operations  15.8 us (3%)
  local copies, waits for them, and re-layouts  9.95 us (2%)
  blocking collectives  5.87 us (1%)
    psum x1, waiting for transfers between devices, body(): left = lax.psum(left_local, 'dp') / replicas  83.7 us
    psum x1, waiting for transfers between devices, body(): right_share = lax.psum(right_share, 'dp') / replicas  76 us
    all_gather x1, waiting for transfers between devices, body(): lax.all_gather(out_grad, 'tensor', axis=0, tiled=True)  38 us
    another operation x6, other arithmetic, orthonormal(): chol = jnp.linalg.cholesky(gram)  34 us
    reduce_scatter x1, waiting for transfers between devices, body(): lax.psum_scatter(contract_rows(columns, ortho), 'tensor', scatter_dimensi...  31.3 us
    psum x1, waiting for transfers between devices, body(): gram = lax.psum(contract_rows(left, left), 'tensor')  28.5 us
    dot_general x2, matrix products, contract_rows(): lax.dot_general(first, second, (((0,), (0,)), ((), ())), precision=HIGH,...  24.9 us
    another operation x4, other arithmetic, orthonormal(): lax.linalg.triangular_solve(chol, left, left_side=False, lower=True, tran...  23.4 us
  transfers between devices with their start and end apart: 7, of which 7 were waited for; matrix products, arithmetic and copies ran while one was open for 4% of the time, Pallas kernels for 0%

commit v1 on v0

--- a/solution.py
+++ b/solution.py
@@ -33,7 +33,7 @@
         precision=HIGH,
         preferred_element_type=jnp.float32,
     )
-    left = lax.psum(left_local, "dp") / replicas
+    left = jnp.sum(lax.all_gather(left_local, "dp"), axis=0) / replicas
     gram = lax.psum(contract_rows(left, left), "tensor")
     ortho = orthonormal(left, gram)
     columns = buffer

time: 458 us -> 522 us (1.14)
  waiting for transfers between devices: 282 us -> 354 us
    all_gather x0 -> x1, waiting for transfers between devices: none -> 151 us  [body(): left = jnp.sum(lax.all_gather(left_local, 'dp'), axis=0) / replicas]
    psum x1 -> x0, waiting for transfers between devices: 83.7 us -> none  [body(): left = lax.psum(left_local, 'dp') / replicas]
  transfers between devices with their start and end apart: 7 -> 7, of which waited for: 7 -> 7; matrix products, arithmetic and copies ran while one was open for 4% -> 3% of each run, Pallas kernels for 0% -> 0%
where the time goes in v1:
time: 522 us; the launch traced here: 514 us
  waiting for transfers between devices  354 us (68%)
  matrix products  68.1 us (13%)
  other arithmetic  62.8 us (12%)
  between operations  15.8 us (3%)
  local copies, waits for them, and re-layouts  6.6 us (1%)
  blocking collectives  5.87 us (1%)
    all_gather x1, waiting for transfers between devices, body(): left = jnp.sum(lax.all_gather(left_local, 'dp'), axis=0) / replicas  151 us
    psum x1, waiting for transfers between devices, body(): right_share = lax.psum(right_share, 'dp') / replicas  75.9 us
    all_gather x1, waiting for transfers between devices, body(): lax.all_gather(out_grad, 'tensor', axis=0, tiled=True)  38 us
    another operation x6, other arithmetic, orthonormal(): chol = jnp.linalg.cholesky(gram)  33.9 us
    reduce_scatter x1, waiting for transfers between devices, body(): lax.psum_scatter(contract_rows(columns, ortho), 'tensor', scatter_dimensi...  31.3 us
    psum x1, waiting for transfers between devices, body(): gram = lax.psum(contract_rows(left, left), 'tensor')  30 us
    dot_general x2, matrix products, contract_rows(): lax.dot_general(first, second, (((0,), (0,)), ((), ())), precision=HIGH,...  23.3 us
    another operation x4, other arithmetic, orthonormal(): lax.linalg.triangular_solve(chol, left, left_side=False, lower=True, tran...  19.8 us
  transfers between devices with their start and end apart: 7, of which 7 were waited for; matrix products, arithmetic and copies ran while one was open for 3% of the time, Pallas kernels for 0%

profile of v1, /device:TPU:0, one launch (start us, length us, event | category | flops | bytes accessed | tf_op | source)
XLA Modules:
  0.0 514.1 jit_solution(8959229517802401319)
XLA Ops:
  7.2 0.0 all-gather.6.cloned.1.call-start
  7.2 0.7 all-gather.6.cloned.1.call-update
  7.9 0.0 all-gather.8.cloned.1.call-start
  8.0 0.7 all-gather.8.cloned.1.call-update
  8.7 0.0 all-gather.12.cloned.1.call-start
  8.7 38.0 %all-gather.6.cloned.1.call-done = bf16[1024,2048]{1,0:T(8,128)(2,1)} async-done(((bf16[256,2048]{1,0:T(8,128)(2,1)}), bf16[1024,2048]{1,0:T(8,128)(2,1)}) %all-gather.6.cloned.1.call-update) | async-done | bytes 4194320 | tf_op jit(solution)/shard_map/all_gather | solution.py:24
  46.8 12.2 %multiply_add_fusion = f32[1280,2048]{1,0:T(8,128)} fusion(f32[1280,2048]{1,0:T(8,128)} %param.6, bf16[1024,1280]{1,0:T(8,128)(2,1)S(1)} %copy-done, bf16[1024,2048]{1,0:T(8,128)(2,1)} %all-gather.6.cloned.1.call-done), kind=kOutput, calls=%fused_computation.3 | convolution fusion | flops 5373952000 | bytes 27787264 | tf_op jit(solution)/shard_map/dot_general | solution.py:22
  58.9 12.0 %all-gather.8.cloned.1.call-done = f32[2048,256]{1,0:T(8,128)} async-done(((f32[512,256]{1,0:T(8,128)}), f32[2048,256]{1,0:T(8,128)}) %all-gather.8.cloned.1.call-update) | async-done | bytes 2097168 | tf_op jit(solution)/shard_map/all_gather | solution.py:32
  70.9 12.5 %fusion.11 = f32[1280,256]{1,0:T(8,128)} fusion(f32[1280,2048]{1,0:T(8,128)} %multiply_add_fusion, f32[2048,256]{1,0:T(8,128)} %all-gather.8.cloned.1.call-done), kind=kOutput, calls=%fused_computation.38 | convolution fusion | flops 8053063680 | bytes 13893632 | tf_op jit(solution)/shard_map/dot_general | solution.py:30
  83.4 0.0 all-reduce.4.cloned.1.call-start
  83.5 150.6 %all-gather.12.cloned.1.call-done = f32[10240,256]{1,0:T(8,128)} async-done(((f32[1280,256]{1,0:T(8,128)}), f32[10240,256]{1,0:T(8,128)}) %all-gather.12.cloned.1.call-update) | async-done | bytes 10485776 | tf_op jit(solution)/shard_map/all_gather | solution.py:36
  234.1 4.8 reduce_sum.18
  238.9 3.0 fusion.8
  241.9 0.0 all-reduce.4.cloned.1.call-update
  241.9 0.5 reduce-scatter.2.cloned.1.call-start
  242.4 0.1 broadcast_multiply_fusion
  242.5 30.0 %all-reduce.4.cloned.1.call-done = f32[256,256]{0,1:T(8,128)} async-done(((f32[256,256]{0,1:T(8,128)}), f32[256,256]{0,1:T(8,128)}) %all-reduce.4.cloned.1.call-update) | async-done | bytes 262160 | tf_op jit(solution)/shard_map/psum | solution.py:37
  272.5 1.1 copy.8
  273.6 1.0 fusion.2
  274.6 11.7 %cholesky.50 = f32[128,128]{1,0:T(8,128)S(1)} custom-call(f32[128,128]{1,0:T(8,128)S(1)} %cholesky.118), custom_call_target="Cholesky" | custom-call | tf_op jit(solution)/shard_map/jit(cholesky)/cholesky | solution.py:16
  286.4 9.8 %custom-call.14 = f32[1,128,128]{1,2,0:T(8,128)S(1)} custom-call(f32[1,128,128]{2,1,0:T(8,128)S(1)} %get-tuple-element.29), custom_call_target="InvertDiagBlocksLowerTriangular" | custom-call | tf_op jit(solution)/shard_map/jit(cholesky)/cholesky | solution.py:16
  296.2 0.2 constant_dynamic-update-slice_fusion.1
  296.4 0.3 convolution_subtract_fusion.1
  296.7 11.7 %cholesky.105 = f32[128,128]{1,0:T(8,128)S(1)} custom-call(f32[128,128]{1,0:T(8,128)S(1)} %convolution_subtract_fusion.1), custom_call_target="Cholesky" | custom-call | tf_op jit(solution)/shard_map/jit(cholesky)/cholesky | solution.py:16
  308.4 0.6 compare_reduce_fusion
  310.4 0.1 triangular_solve.58
  310.5 4.2 while.1
  310.7 0.6 fusion.23
  311.3 1.4 bitcast_dynamic-update-slice_fusion.2
  312.7 0.6 fusion.23
  313.3 1.4 bitcast_dynamic-update-slice_fusion.2
  314.7 19.7 %custom-call.15 = f32[2,128,128]{1,2,0:T(8,128)S(1)} custom-call(f32[2,128,128]{2,1,0:T(8,128)S(1)} %get-tuple-element.10), custom_call_target="InvertDiagBlocksLowerTriangular" | custom-call | tf_op jit(solution)/shard_map/triangular_solve | solution.py:17
  334.3 0.7 fusion
  335.1 1.2 convolution_subtract_fusion
  336.3 0.7 fusion.3
  337.0 20.3 %fusion.9 = f32[2048,256]{1,0:T(8,128)} fusion(f32[1280,2048]{1,0:T(8,128)} %multiply_add_fusion, f32[1280,128]{0,1:T(8,128)S(1)} %fusion.3, f32[1280,128]{0,1:T(8,128)S(1)} %fusion), kind=kOutput, calls=%fused_computation.36 | convolution fusion | flops 8053391360 | bytes 13893632 | tf_op jit(solution)/shard_map/dot_general | solution.py:10
  357.3 0.0 reduce-scatter.2.cloned.1.call-update
  357.4 0.0 all-reduce.6.cloned.1.call-start
  357.4 31.3 %reduce-scatter.2.cloned.1.call-done = f32[512,256]{1,0:T(8,128)} async-done(((f32[2048,256]{1,0:T(8,128)}), f32[512,256]{1,0:T(8,128)}) %reduce-scatter.2.cloned.1.call-update) | async-done | bytes 524304 | tf_op jit(solution)/shard_map/reduce_scatter | solution.py:40
  388.7 0.0 all-gather.10.cloned.1.call-start
  388.8 75.9 %all-reduce.6.cloned.1.call-done = f32[512,256]{1,0:T(8,128)} async-done(((f32[512,256]{1,0:T(8,128)}), f32[512,256]{1,0:T(8,128)}) %all-reduce.6.cloned.1.call-update) | async-done | bytes 524304 | tf_op jit(solution)/shard_map/psum | solution.py:43
  464.7 1.1 multiply_reduce_fusion
  465.8 5.9 %psum.23 = f32[1,256]{1,0:T(1,128)S(1)} all-reduce(f32[1,256]{1,0:T(1,128)S(1)} %bitcast.41), channel_id=1, replica_groups=mesh['dp'=8,'tensor'=4] {'tensor'}, use_global_device_ids=true, to_apply=%region_9.10 | all-reduce | flops 256 | bytes 2048 | tf_op jit(solution)/shard_map/psum | solution.py:44
  471.7 2.0 broadcast_multiply_fusion.1
  473.7 0.1 pad_maximum_fusion
  473.8 1.5 copy.9
  475.3 14.7 %all-gather.10.cloned.1.call-done = bf16[2048,256]{1,0:T(8,128)(2,1)} async-done(((bf16[512,256]{1,0:T(8,128)(2,1)}), bf16[2048,256]{1,0:T(8,128)(2,1)}) %all-gather.10.cloned.1.call-update) | async-done | bytes 1048592 | tf_op jit(solution)/shard_map/all_gather | solution.py:49
  490.0 17.1 %multiply_subtract_fusion = f32[1280,2048]{1,0:T(8,128)} fusion(f32[1280,2048]{1,0:T(8,128)} %multiply_add_fusion, bf16[2048,256]{1,0:T(8,128)(2,1)} %all-gather.10.cloned.1.call-done, f32[1280,128]{0,1:T(8,128)} %copy-done.2, f32[1280,128]{0,1:T(8,128)S(1)} %fusion), kind=kOutput, calls=%fused_computation.2 | convolution fusion | flops 8058634240 | bytes 23330816 | tf_op jit(solution)/shard_map/dot_general | solution.py:47
  (19 shorter events, 0.2 us)
Async XLA Ops:
  7.2 39.6 %copy-start = (bf16[1024,1280]{1,0:T(8,128)(2,1)S(1)}, bf16[1024,1280]{1,0:T(8,128)(2,1)}, u32[]{:S(2)}) copy-start(bf16[1024,1280]{1,0:T(8,128)(2,1)} %param.4) | copy-start | bytes 7864324
  7.2 39.6 %all-gather.6.cloned.1.call-start = ((), (), s32[]{:S(2)}) async-start(), calls=%async_computation.1 | async-start | bytes 5242880 | tf_op jit(solution)/shard_map/all_gather | solution.py:24
  7.9 63.0 %all-gather.8.cloned.1.call-start = ((), (), s32[]{:S(2)}) async-start(), calls=%async_computation.2 | async-start | bytes 2621440 | tf_op jit(solution)/shard_map/all_gather | solution.py:32
  8.7 225.4 %all-gather.12.cloned.1.call-start = ((), (), s32[]{:S(2)}) async-start(), calls=%async_computation.7 | async-start | bytes 11796480 | tf_op jit(solution)/shard_map/all_gather | solution.py:36
  83.4 189.1 %all-reduce.4.cloned.1.call-start = ((), (), s32[]{:S(2)}) async-start(), calls=%async_computation.3 | async-start | bytes 524288 | tf_op jit(solution)/shard_map/psum | solution.py:37
  241.9 146.8 %reduce-scatter.2.cloned.1.call-start = ((), (), s32[]{:S(2)}) async-start(), calls=%async_computation.4 | async-start | bytes 2621440 | tf_op jit(solution)/shard_map/reduce_scatter | solution.py:40
  337.0 136.7 %copy-start.2 = (f32[1280,128]{0,1:T(8,128)}, f32[1280,128]{0,1:T(8,128)S(1)}, u32[]{:S(2)}) copy-start(f32[1280,128]{0,1:T(8,128)S(1)} %fusion.3) | copy-start | bytes 1966084
  357.4 107.3 %all-reduce.6.cloned.1.call-start = ((), (), s32[]{:S(2)}) async-start(), calls=%async_computation.5 | async-start | bytes 1048576 | tf_op jit(solution)/shard_map/psum | solution.py:43
  388.7 101.3 %all-gather.10.cloned.1.call-start = ((), (), s32[]{:S(2)}) async-start(), calls=%async_computation.6 | async-start | bytes 1310720 | tf_op jit(solution)/shard_map/all_gather | solution.py:49
  490.0 17.1 %copy-start.1 = (bf16[1024,1280]{1,0:T(8,128)(2,1)S(1)}, bf16[1024,1280]{1,0:T(8,128)(2,1)}, u32[]{:S(2)}) copy-start(bf16[1024,1280]{1,0:T(8,128)(2,1)} %param.4) | copy-start | bytes 7864324
Sparse Core Ops, SparseCore 0:
  9.5 37.1 all-gather.5
  48.3 22.5 all-gather.7
  83.5 150.5 all-gather.11
  242.0 30.4 all-reduce.3
  357.5 31.1 reduce-scatter.1
  392.0 72.6 all-reduce.5
  473.8 16.1 all-gather.9
